TPU v7x, 32 devices: a whole 2x2x4 slice. The times are simulated.
32 devices in a mesh: act: 8 (over z, x), rep: 4 (over y, core).
Axes of the slice: x: 2, y: 2, z: 4, core: 2. Of those that a mesh axis runs over, the one named last changes fastest.
Arguments:
- estimated_returns: float32 [512, 16384], P('act', 'rep'), may hold values from -1000 to 1000
- chosen_move_ids: int32 [512, 16384], P('act', 'rep'), may hold values from 0 to 17
- previous_eta: float32 [1], replicated, may hold values from 0.3 to 3
- trust_region_epsilon: float32 [1], replicated, may hold values from 0.02 to 1
Outputs:
- sample_importance: float32 [512, 16384], P('act', 'rep')
- goal_distribution: float32 [18, 16384], P(None, ('rep', 'act'))
- new_temperature: float32 [1], replicated
All inputs are finite; a program needn't handle non-finite values.
Results may differ from a plain program's by a relative error of at most 0.0003.
Values sent between devices are 32-bit elements; how exact they have to be, the bound alone decides.
A program may use at most 64 MiB of HBM per device.

v0:
```python
import jax
import jax.numpy as jnp
from jax import lax
from jax.sharding import PartitionSpec as P

NACT = 18
ITERS = 3


def summary_figures(centered_returns, lagrange_eta):
    exponential_term = jnp.exp(centered_returns / lagrange_eta)
    partition_total = jnp.sum(exponential_term, axis=0)
    leading_part = jnp.sum(exponential_term * centered_returns, axis=0)
    trailing_part = jnp.sum(exponential_term * centered_returns * centered_returns, axis=0)
    return (exponential_term, partition_total, leading_part, trailing_part)


def within_situation(partition_total, leading_part, trailing_part, lagrange_eta, move_draws):
    entropy_gap = (
        leading_part / (partition_total * lagrange_eta)
        - jnp.log(partition_total)
        + jnp.log(jnp.float32(move_draws))
    )
    mean_first = leading_part / partition_total
    spread = trailing_part / partition_total - mean_first * mean_first
    return (jnp.sum(entropy_gap), jnp.sum(spread))


def gradient_step(lagrange_eta, ceiling_term, aggregate_relative_entropy, aggregate_deviation):
    change_amount = (
        (ceiling_term - aggregate_relative_entropy)
        * lagrange_eta
        / (1.0 + aggregate_deviation / lagrange_eta)
    )
    return lagrange_eta * jnp.exp(-jnp.tanh(change_amount))


def per_action(probs, ids_block):
    return jnp.stack([jnp.sum(jnp.where(ids_block == k, probs, 0.0), axis=0) for k in range(NACT)])


def scatter_target(probs, ids_block):
    return lax.psum_scatter(per_action(probs, ids_block), "act", scatter_dimension=1, tiled=True)


def on_device(estimated_returns, chosen_move_ids, previous_eta, trust_region_epsilon):
    lagrange_eta = previous_eta[0]
    ceiling_term = trust_region_epsilon[0]
    move_draws = estimated_returns.shape[0] * lax.axis_size("act")
    q_rows = lax.all_to_all(estimated_returns, "act", split_axis=1, concat_axis=0, tiled=True)
    tally_number = q_rows.shape[1] * lax.axis_size("act") * lax.axis_size("rep")
    centered_returns = q_rows - jnp.max(q_rows, axis=0, keepdims=True)
    for step in range(ITERS):
        exponential_term, partition_total, leading_part, trailing_part = summary_figures(
            centered_returns, lagrange_eta
        )
        shard_divergence, shard_value_spread = within_situation(
            partition_total, leading_part, trailing_part, lagrange_eta, move_draws
        )
        aggregate_relative_entropy, aggregate_deviation = lax.psum(
            (shard_divergence, shard_value_spread), ("act", "rep")
        )
        lagrange_eta = gradient_step(
            lagrange_eta,
            ceiling_term,
            aggregate_relative_entropy / tally_number,
            aggregate_deviation / tally_number,
        )
    exponential_term, partition_total, leading_part, trailing_part = summary_figures(
        centered_returns, lagrange_eta
    )
    probs_rows = exponential_term / partition_total
    sample_importance = lax.all_to_all(
        move_draws * probs_rows, "act", split_axis=0, concat_axis=1, tiled=True
    )
    goal_distribution = scatter_target(sample_importance / jnp.float32(move_draws), chosen_move_ids)
    return (sample_importance, goal_distribution, jnp.reshape(lagrange_eta, (1,)))


def solution(mesh):
    in_specs = (P("act", "rep"), P("act", "rep"), P(), P())
    out_specs = (P("act", "rep"), P(None, ("rep", "act")), P())
    return jax.shard_map(
        on_device, mesh=mesh, in_specs=in_specs, out_specs=out_specs, check_vma=False
    )
```

profile of v0, /device:TPU:0, one launch (start us, length us, event | category | flops | bytes accessed | tf_op | source)
XLA Modules:
  0.0 275.7 jit_solution(3576206588471246463)
XLA Ops:
  7.2 2.3 copy.12
  9.4 7.3 %all-to-all-start = ((f32[64,8,512]{2,0,1:T(8,128)}), f32[64,8,512]{2,0,1:T(8,128)S(1)}, u32[]{:S(2)}, u32[]{:S(2)}) async-start(f32[64,8,512]{2,0,1:T(8,128)} %bitcast.86), calls=%async_computation | async-start | bytes 2097152 | tf_op jit(solution)/shard_map/all_to_all | solution.py:50
  16.7 0.0 reduce-scatter.2.cloned.1.call-start
  18.1 24.4 %all-to-all-done = f32[64,8,512]{2,0,1:T(8,128)S(1)} async-done(((f32[64,8,512]{2,0,1:T(8,128)}), f32[64,8,512]{2,0,1:T(8,128)S(1)}, u32[]{:S(2)}, u32[]{:S(2)}) %all-to-all-start) | async-done | bytes 1048608 | tf_op jit(solution)/shard_map/all_to_all | solution.py:50
  42.5 0.1 reduce_max.9
  42.6 0.3 fusion.1
  42.9 0.7 subtract_reduce_fusion.2
  43.6 38.0 %all-reduce.2 = (f32[]{:T(128)}, f32[]{:T(128)}) all-reduce(f32[]{:T(128)} %get-tuple-element.35, f32[]{:T(128)} %get-tuple-element.34), channel_id=1, replica_groups=mesh['act'=8,'rep'=4] {'act','rep'}, use_global_device_ids=true, to_apply=%region_4.0 | all-reduce | flops 2 | bytes 16 | tf_op jit(solution)/shard_map/psum | solution.py:60
  83.0 0.3 fusion.3
  83.3 0.6 subtract_reduce_fusion.1
  84.0 41.8 %all-reduce.1 = (f32[]{:T(128)}, f32[]{:T(128)}) all-reduce(f32[]{:T(128)} %get-tuple-element.33, f32[]{:T(128)} %get-tuple-element.32), channel_id=1, replica_groups=mesh['act'=8,'rep'=4] {'act','rep'}, use_global_device_ids=true, to_apply=%region_11.0 | all-reduce | flops 2 | bytes 16 | tf_op jit(solution)/shard_map/psum | solution.py:60
  127.2 0.3 fusion.5
  127.6 0.6 subtract_reduce_fusion
  128.2 39.7 %all-reduce = (f32[]{:T(128)}, f32[]{:T(128)}) all-reduce(f32[]{:T(128)} %get-tuple-element.31, f32[]{:T(128)} %get-tuple-element.30), channel_id=1, replica_groups=mesh['act'=8,'rep'=4] {'act','rep'}, use_global_device_ids=true, to_apply=%region_18.0 | all-reduce | flops 2 | bytes 16 | tf_op jit(solution)/shard_map/psum | solution.py:60
  169.3 0.2 fusion.13
  169.5 0.2 divide_multiply_fusion
  169.8 29.3 %all_to_all.29 = f32[8,64,512]{2,1,0:T(8,128)S(1)} all-to-all(f32[8,64,512]{2,1,0:T(8,128)S(1)} %divide_multiply_fusion), channel_id=1, replica_groups=mesh['act'=8,'rep'=4] {'act'}, dimensions={0} | all-to-all | bytes 2097152 | tf_op jit(solution)/shard_map/all_to_all | solution.py:73
  199.0 0.0 copy-start.1
  199.0 0.1 copy.10
  199.1 0.0 copy-start
  199.1 1.5 copy-done.1
  200.6 2.7 select_reduce_fusion
  203.4 0.0 copy-done
  203.4 2.4 stack.75
  205.7 0.0 reduce-scatter.2.cloned.1.call-update
  205.8 62.0 %reduce-scatter.2.cloned.1.call-done = f32[18,512]{1,0:T(8,128)} async-done(((f32[18,4096]{1,0:T(8,128)}), f32[18,512]{1,0:T(8,128)}) %reduce-scatter.2.cloned.1.call-update) | async-done | bytes 36880 | tf_op jit(solution)/shard_map/reduce_scatter | solution.py:43
Async XLA Ops:
  9.4 33.0 %all-to-all-start = ((f32[64,8,512]{2,0,1:T(8,128)}), f32[64,8,512]{2,0,1:T(8,128)S(1)}, u32[]{:S(2)}, u32[]{:S(2)}) async-start(f32[64,8,512]{2,0,1:T(8,128)} %bitcast.86), calls=%async_computation | async-start | bytes 2097152 | tf_op jit(solution)/shard_map/all_to_all | solution.py:50
  16.7 251.0 %reduce-scatter.2.cloned.1.call-start = ((), (), s32[]{:S(2)}) async-start(), calls=%async_computation.3 | async-start | bytes 442368 | tf_op jit(solution)/shard_map/reduce_scatter | solution.py:43
  199.0 1.6 copy-start.1
  199.1 4.2 %copy-start = (f32[8,8,8,512]{3,2,0,1:T(8,128)}, f32[8,8,8,512]{3,2,0,1:T(8,128)S(1)}, u32[]{:S(2)}) copy-start(f32[8,8,8,512]{3,2,0,1:T(8,128)S(1)} %copy.10) | copy-start | bytes 3145732
Sparse Core Ops, SparseCore 0:
  205.9 61.8 reduce-scatter.1
where the time goes:
time: 277 us; the launch traced here: 276 us
  blocking collectives  149 us (54%)
  waiting for transfers between devices  86.4 us (31%)
  between operations  20.8 us (8%)
  starting transfers between devices  7.32 us (3%)
  local copies, waits for them, and re-layouts  6.25 us (2%)
  other arithmetic  6.15 us (2%)
    psum x3, blocking collectives, on_device(): lax.psum((shard_divergence, shard_value_spread), ('act', 'rep'))  119 us
    reduce_scatter x1, waiting for transfers between devices, scatter_target(): lax.psum_scatter(per_action(probs, ids_block), 'act', scatter_dimension=1...  62 us
    all_to_all x1, blocking collectives, on_device(): lax.all_to_all(move_draws * probs_rows, 'act', split_axis=0, concat_axis=...  29.3 us
    all_to_all x1, waiting for transfers between devices, on_device(): lax.all_to_all(estimated_returns, 'act', split_axis=1, concat_axis=0, til...  24.4 us
    all_to_all x1, starting transfers between devices, on_device(): lax.all_to_all(estimated_returns, 'act', split_axis=1, concat_axis=0, til...  7.28 us
  transfers between devices with their start and end apart: 2, of which 2 were waited for; matrix products, arithmetic and copies ran while one was open for 0% of the time, Pallas kernels for 0%

commit v1 on v0

--- a/solution.py
+++ b/solution.py
@@ -47,7 +47,10 @@
     lagrange_eta = previous_eta[0]
     ceiling_term = trust_region_epsilon[0]
     move_draws = estimated_returns.shape[0] * lax.axis_size("act")
-    q_rows = lax.all_to_all(estimated_returns, "act", split_axis=1, concat_axis=0, tiled=True)
+    size = lax.axis_size("act")
+    blocks = jnp.stack(jnp.split(estimated_returns, size, axis=1), axis=0)
+    blocks = lax.all_to_all(blocks, "act", split_axis=0, concat_axis=0)
+    q_rows = jnp.concatenate(blocks, axis=0)
     tally_number = q_rows.shape[1] * lax.axis_size("act") * lax.axis_size("rep")
     centered_returns = q_rows - jnp.max(q_rows, axis=0, keepdims=True)
     for step in range(ITERS):

time: 277 us -> 287 us (1.036)
  local copies, waits for them, and re-layouts: 6.25 us -> 16.5 us
    unnamed x4 -> x11, local copies, waits for them, and re-layouts: 1.51 us -> 12.5 us
where the time goes in v1:
time: 287 us; the launch traced here: 286 us
  blocking collectives  149 us (52%)
  waiting for transfers between devices  86.4 us (30%)
  between operations  20.8 us (7%)
  local copies, waits for them, and re-layouts  16.5 us (6%)
  starting transfers between devices  7.32 us (3%)
  other arithmetic  6.15 us (2%)
    psum x3, blocking collectives, on_device(): lax.psum((shard_divergence, shard_value_spread), ('act', 'rep'))  119 us
    reduce_scatter x1, waiting for transfers between devices, scatter_target(): lax.psum_scatter(per_action(probs, ids_block), 'act', scatter_dimension=1...  62 us
    all_to_all x1, blocking collectives, on_device(): lax.all_to_all(move_draws * probs_rows, 'act', split_axis=0, concat_axis=...  29.3 us
    all_to_all x1, waiting for transfers between devices, on_device(): blocks = lax.all_to_all(blocks, 'act', split_axis=0, concat_axis=0)  24.4 us
    unnamed x11, local copies, waits for them, and re-layouts  12.5 us
    all_to_all x1, starting transfers between devices, on_device(): blocks = lax.all_to_all(blocks, 'act', split_axis=0, concat_axis=0)  7.28 us
  transfers between devices with their start and end apart: 2, of which 2 were waited for; matrix products, arithmetic and copies ran while one was open for 0% of the time, Pallas kernels for 0%

profile of v1, /device:TPU:0, one launch (start us, length us, event | category | flops | bytes accessed | tf_op | source)
XLA Modules:
  0.0 286.0 jit_solution(5960351318621241986)
XLA Ops:
  7.2 1.6 bitcast_dynamic-update-slice_fusion.7
  8.7 1.6 bitcast_dynamic-update-slice_fusion.6
  10.3 1.6 bitcast_dynamic-update-slice_fusion.5
  11.9 1.6 bitcast_dynamic-update-slice_fusion.4
  13.4 1.6 bitcast_dynamic-update-slice_fusion.3
  15.0 1.6 bitcast_dynamic-update-slice_fusion.2
  16.6 1.6 bitcast_dynamic-update-slice_fusion.1
  18.1 1.6 bitcast_dynamic-update-slice_fusion
  19.7 7.3 %all-to-all-start = ((f32[8,64,512]{2,1,0:T(8,128)}), f32[8,64,512]{2,1,0:T(8,128)S(1)}, u32[]{:S(2)}, u32[]{:S(2)}) async-start(f32[8,64,512]{2,1,0:T(8,128)} %bitcast_dynamic-update-slice_fusion), calls=%async_computation | async-start | bytes 2097152 | tf_op jit(solution)/shard_map/all_to_all | solution.py:52
  27.0 0.0 reduce-scatter.2.cloned.1.call-start
  28.3 24.4 %all-to-all-done = f32[8,64,512]{2,1,0:T(8,128)S(1)} async-done(((f32[8,64,512]{2,1,0:T(8,128)}), f32[8,64,512]{2,1,0:T(8,128)S(1)}, u32[]{:S(2)}, u32[]{:S(2)}) %all-to-all-start) | async-done | bytes 1048608 | tf_op jit(solution)/shard_map/all_to_all | solution.py:52
  52.8 0.1 reduce_max.9
  52.9 0.3 multiply_reduce_fusion.2
  53.2 0.7 subtract_reduce_fusion.2
  53.9 38.0 %all-reduce.2 = (f32[]{:T(128)}, f32[]{:T(128)}) all-reduce(f32[]{:T(128)} %get-tuple-element.35, f32[]{:T(128)} %get-tuple-element.34), channel_id=1, replica_groups=mesh['act'=8,'rep'=4] {'act','rep'}, use_global_device_ids=true, to_apply=%region_4.0 | all-reduce | flops 2 | bytes 16 | tf_op jit(solution)/shard_map/psum | solution.py:63
  93.3 0.3 multiply_reduce_fusion.1
  93.6 0.6 subtract_reduce_fusion.1
  94.2 41.8 %all-reduce.1 = (f32[]{:T(128)}, f32[]{:T(128)}) all-reduce(f32[]{:T(128)} %get-tuple-element.33, f32[]{:T(128)} %get-tuple-element.32), channel_id=1, replica_groups=mesh['act'=8,'rep'=4] {'act','rep'}, use_global_device_ids=true, to_apply=%region_11.0 | all-reduce | flops 2 | bytes 16 | tf_op jit(solution)/shard_map/psum | solution.py:63
  137.5 0.3 multiply_reduce_fusion
  137.8 0.6 subtract_reduce_fusion
  138.4 39.7 %all-reduce = (f32[]{:T(128)}, f32[]{:T(128)}) all-reduce(f32[]{:T(128)} %get-tuple-element.31, f32[]{:T(128)} %get-tuple-element.30), channel_id=1, replica_groups=mesh['act'=8,'rep'=4] {'act','rep'}, use_global_device_ids=true, to_apply=%region_18.0 | all-reduce | flops 2 | bytes 16 | tf_op jit(solution)/shard_map/psum | solution.py:63
  179.6 0.2 fusion.3
  179.8 0.2 divide_multiply_fusion
  180.0 29.3 %all_to_all.21 = f32[8,64,512]{2,1,0:T(8,128)S(1)} all-to-all(f32[8,64,512]{2,1,0:T(8,128)S(1)} %divide_multiply_fusion), channel_id=1, replica_groups=mesh['act'=8,'rep'=4] {'act'}, dimensions={0} | all-to-all | bytes 2097152 | tf_op jit(solution)/shard_map/all_to_all | solution.py:76
  209.3 0.0 copy-start.1
  209.3 0.1 copy.8
  209.4 0.0 copy-start
  209.4 1.5 copy-done.1
  210.9 2.7 select_reduce_fusion
  213.6 0.0 copy-done
  213.6 2.4 stack.111
  216.0 0.0 reduce-scatter.2.cloned.1.call-update
  216.0 62.0 %reduce-scatter.2.cloned.1.call-done = f32[18,512]{1,0:T(8,128)} async-done(((f32[18,4096]{1,0:T(8,128)}), f32[18,512]{1,0:T(8,128)}) %reduce-scatter.2.cloned.1.call-update) | async-done | bytes 36880 | tf_op jit(solution)/shard_map/reduce_scatter | solution.py:43
Async XLA Ops:
  19.7 33.0 %all-to-all-start = ((f32[8,64,512]{2,1,0:T(8,128)}), f32[8,64,512]{2,1,0:T(8,128)S(1)}, u32[]{:S(2)}, u32[]{:S(2)}) async-start(f32[8,64,512]{2,1,0:T(8,128)} %bitcast_dynamic-update-slice_fusion), calls=%async_computation | async-start | bytes 2097152 | tf_op jit(solution)/shard_map/all_to_all | solution.py:52
  27.0 251.0 %reduce-scatter.2.cloned.1.call-start = ((), (), s32[]{:S(2)}) async-start(), calls=%async_computation.3 | async-start | bytes 442368 | tf_op jit(solution)/shard_map/reduce_scatter | solution.py:43
  209.3 1.6 copy-start.1
  209.4 4.2 %copy-start = (f32[8,8,8,512]{3,2,0,1:T(8,128)}, f32[8,8,8,512]{3,2,0,1:T(8,128)S(1)}, u32[]{:S(2)}) copy-start(f32[8,8,8,512]{3,2,0,1:T(8,128)S(1)} %copy.8) | copy-start | bytes 3145732
Sparse Core Ops, SparseCore 0:
  216.1 61.8 reduce-scatter.1
